TPU v7x, 128 devices: a whole 4x4x4 slice. The times are simulated.
128 devices in a mesh: row: 8 (over x_hi, y), col: 16 (over x_lo, z, core).
Axes of the slice: x: 4 (x_hi: 2, x_lo: 2; x = x_hi * 2 + x_lo), y: 4, z: 4, core: 2. Of those that a mesh axis runs over, the one named last changes fastest.
Arguments:
- basis: bfloat16 [40, 524288], P(None, ('row', 'col'))
- expand: float32 [3, 8, 40], replicated, may hold values from -1 to 1
- tiles: bfloat16 [3, 24576, 128, 128], P(None, ('row', 'col')), may hold values from -0.21875 to 0.21875
- tile_rows: int32 [24576], P(('row', 'col')), may hold values from 0 to 511, as said below
- tile_cols: int32 [24576], P(('row', 'col')), may hold values from 0 to 255
Outputs:
- new_block: float32 [8, 524288], P(None, ('row', 'col'))
- coefficients: float32 [8, 40], replicated
- factor: float32 [8, 8], replicated
Inputs may be any that keep to these rules, and one draw needn't show every extreme that they name: `tile_rows`: each device's 192 tiles come in 16 runs of 12; the row tiles of run k are 12 distinct values from k * 32 to (k + 1) * 32 - 1.
All inputs are finite; a program needn't handle non-finite values.
Results may differ from a plain program's by a relative error of at most 0.0054.
Values may be sent and summed in bfloat16 or wider, within the bound.
A program may use at most 64 MiB of HBM per device.

v0:
```python
import math

import jax
import jax.numpy as jnp
from jax import lax
from jax.sharding import Mesh
from jax.sharding import PartitionSpec as P

ROW = ("row_0", "row_1")
COL = ("col_0", "col_1", "col_2")
ROW_COL = ("row_0", "row_1", "col_0", "col_1", "col_2")


def from_everyone(value, axis):
    copies = jnp.broadcast_to(value, (lax.axis_size(axis), *value.shape))
    return lax.all_to_all(copies, axis, split_axis=0, concat_axis=0, tiled=True)


def joined_along(blocks, dim):
    blocks = jnp.moveaxis(blocks, 0, dim)
    shape = blocks.shape
    return blocks.reshape(*shape[:dim], shape[dim] * shape[dim + 1], *shape[dim + 2 :])


def collect(value, axis, dim):
    blocks = from_everyone(value, axis)
    return joined_along(blocks, dim)


def by_axis(value, axes):
    for axis in axes:
        value = lax.psum(value, axis)
    return value


def shards(basis, expand, tiles, tile_rows, tile_cols):
    highest = lax.Precision.HIGHEST
    row_count = lax.axis_size(ROW)
    col_count = lax.axis_size(COL)
    krylov, length = basis.shape
    tile_size = tiles.shape[2]
    tile_count = tiles.shape[1]
    block_size = expand.shape[1]
    entries = length * row_count * col_count
    inverse_root = 1.0 / math.sqrt(entries)
    region = length // tile_size
    basis_full = basis.astype(jnp.float32)
    series = jnp.einsum("mbk,kn->mbn", expand, basis_full, precision=highest).astype(jnp.bfloat16)
    gathered = collect(series, ROW, 2)
    col_tiles = gathered.reshape(3, block_size, row_count * length // tile_size, tile_size)
    picked = jnp.take(col_tiles, tile_cols, axis=2)
    products = jnp.einsum("mtij,mbtj->bti", tiles, picked, preferred_element_type=jnp.float32)
    per_owner = tile_count // col_count
    outgoing = products.reshape(block_size, col_count, per_owner * tile_size)
    row_ids = tile_rows.reshape(1, col_count, per_owner)
    incoming, arrived_ids = (
        lax.all_to_all(
            outgoing.astype(jnp.bfloat16), COL, split_axis=1, concat_axis=1, tiled=True
        ).astype(outgoing.dtype),
        lax.all_to_all(row_ids, COL, split_axis=1, concat_axis=1, tiled=True),
    )
    local_rows = arrived_ids.reshape(col_count * per_owner) - lax.axis_index(COL) * region
    onehot = (local_rows[:, None] == jnp.arange(region, dtype=jnp.int32)[None, :]).astype(
        jnp.float32
    )
    received = incoming.reshape(block_size, col_count * per_owner, tile_size)
    applied = jnp.einsum("ts,bti->bsi", onehot, received, precision=highest).reshape(
        block_size, length
    )
    raw_proj = jnp.dot(applied, basis_full.T, precision=highest) * inverse_root
    correlation = jnp.dot(basis_full, basis_full.T, precision=highest) / entries
    energy = jnp.dot(applied, applied.T, precision=highest)
    first_pass, correlation, energy = (
        by_axis(raw_proj, ROW_COL),
        by_axis(correlation, ROW_COL),
        by_axis(energy, ROW_COL),
    )
    second_pass = first_pass - jnp.dot(first_pass, correlation, precision=highest)
    coefficients = first_pass + second_pass
    mixed = jnp.dot(first_pass, coefficients.T, precision=highest)
    curved = jnp.dot(
        jnp.dot(coefficients, correlation, precision=highest), coefficients.T, precision=highest
    )
    gram_block = (energy - mixed - mixed.T + curved) / entries
    cleaned = applied - jnp.dot(coefficients, basis_full, precision=highest) * inverse_root
    factor = jnp.linalg.cholesky(gram_block)
    new_block = lax.linalg.triangular_solve(factor, cleaned, left_side=True, lower=True)
    return (new_block, coefficients, factor)


def solution(mesh):
    finer = Mesh(mesh.devices.reshape(2, 4, 2, 4, 2), ("row_0", "row_1", "col_0", "col_1", "col_2"))
    return jax.shard_map(
        shards,
        mesh=finer,
        in_specs=(P(None, ROW_COL), P(), P(None, ROW_COL, None, None), P(ROW_COL), P(ROW_COL)),
        out_specs=(P(None, ROW_COL), P(), P()),
        check_vma=False,
    )
```

profile of v0, /device:TPU:1, one launch (start us, length us, event | category | flops | bytes accessed | tf_op | source)
XLA Modules:
  0.0 128.4 jit_solution(5950030648145477739)
XLA Ops:
  0.6 1.0 copy-done
  1.6 1.0 convolution_convert_fusion
  2.6 1.3 %broadcast_in_dim.20 = bf16[8,3,8,4096]{3,2,1,0:T(8,128)(2,1)} broadcast(bf16[3,8,4096]{2,1,0:T(8,128)(2,1)S(1)} %convolution_convert_fusion), dimensions={1,2,3} | broadcast | bytes 1769472 | tf_op jit(solution)/shard_map/broadcast_in_dim | solution.py:15
  4.0 7.6 %all-to-all-start = ((bf16[8,3,8,4096]{3,2,1,0:T(8,128)(2,1)}), bf16[8,3,8,4096]{3,2,1,0:T(8,128)(2,1)S(1)}, u32[]{:S(2)}, u32[]{:S(2)}) async-start(bf16[8,3,8,4096]{3,2,1,0:T(8,128)(2,1)} %broadcast_in_dim.20), calls=%async_computation | async-start | bytes 3145728 | tf_op jit(solution)/shard_map/all_to_all | solution.py:16
  11.6 0.7 reshape.40
  12.3 19.8 %all-to-all-done = bf16[8,3,8,4096]{3,2,1,0:T(8,128)(2,1)S(1)} async-done(((bf16[8,3,8,4096]{3,2,1,0:T(8,128)(2,1)}), bf16[8,3,8,4096]{3,2,1,0:T(8,128)(2,1)S(1)}, u32[]{:S(2)}, u32[]{:S(2)}) %all-to-all-start) | async-done | bytes 1572896 | tf_op jit(solution)/shard_map/all_to_all | solution.py:16
  32.1 6.6 %all-to-all-start.2 = ((s32[1,16,12]{2,0,1:T(1,128)}), s32[1,16,12]{2,0,1:T(1,128)S(1)}, u32[]{:S(2)}, u32[]{:S(2)}) async-start(s32[1,16,12]{2,0,1:T(1,128)} %bitcast.7), calls=%async_computation.2 | async-start | bytes 16384 | tf_op jit(solution)/shard_map/all_to_all | solution.py:60
  38.7 0.9 copy.26
  39.5 0.8 reshape_reshape.3
  40.3 1.0 copy.27
  41.3 1.0 gather_fusion
  42.4 11.3 %fusion.6 = bf16[192,8,128]{2,1,0:T(8,128)(2,1)} fusion(bf16[3,192,128,128]{3,2,1,0:T(8,128)(2,1)} %param.7, bf16[192,3,8,128]{3,2,1,0:T(8,128)(2,1)S(1)} %gather_fusion, pred[192]{0:T(512)(128)(4,1)S(1)} %compare_and_fusion), kind=kOutput, calls=%fused_computation.7 | convolution fusion | flops 151781376 | bytes 20447424 | tf_op jit(solution)/shard_map/mtij,mbtj->bti/dot_general | solution.py:52
  53.6 5.7 %all-to-all-start.1 = ((bf16[8,16,1536]{2,0,1:T(8,128)(2,1)}), bf16[8,16,1536]{2,0,1:T(8,128)(2,1)S(1)}, u32[]{:S(2)}, u32[]{:S(2)}) async-start(bf16[8,16,1536]{2,0,1:T(8,128)(2,1)} %bitcast.6), calls=%async_computation.1 | async-start | bytes 786432 | tf_op jit(solution)/shard_map/all_to_all | solution.py:57
  59.4 0.2 convolution_multiply_fusion.1
  59.7 7.9 %all-to-all-done.1 = bf16[8,16,1536]{2,0,1:T(8,128)(2,1)S(1)} async-done(((bf16[8,16,1536]{2,0,1:T(8,128)(2,1)}), bf16[8,16,1536]{2,0,1:T(8,128)(2,1)S(1)}, u32[]{:S(2)}, u32[]{:S(2)}) %all-to-all-start.1) | async-done | bytes 393248 | tf_op jit(solution)/shard_map/all_to_all | solution.py:57
  67.7 0.5 reshape.39
  68.2 0.2 fusion.20
  68.4 0.4 convolution_multiply_fusion.2
  68.8 0.4 convolution_bitcast_fusion
  69.2 9.6 %all-reduce.4 = (f32[8,40]{1,0:T(8,128)S(1)}, f32[40,40]{1,0:T(8,128)S(1)}, f32[8,8]{0,1:T(8,128)S(1)}) all-reduce(f32[8,40]{1,0:T(8,128)S(1)} %convolution_multiply_fusion.2, f32[40,40]{1,0:T(8,128)S(1)} %convolution_multiply_fusion.1, ...), channel_id=1, replica_groups=mesh['row_0'=2,'row_1'=4,'col_0'=2,'col_1'=4,'col_2'=2] {'row_0'}, use_global_device_ids=true, to_apply=%region_5.6 | all-reduce | flops 1984 | bytes 15872 | tf_op jit(solution)/shard_map/psum | solution.py:32
  78.8 12.2 %all-reduce.1 = (f32[8,40]{1,0:T(8,128)S(1)}, f32[40,40]{1,0:T(8,128)S(1)}, f32[8,8]{0,1:T(8,128)S(1)}) all-reduce(f32[8,40]{1,0:T(8,128)S(1)} %get-tuple-element.15, f32[40,40]{1,0:T(8,128)S(1)} %get-tuple-element.16, f32[8,8]{0,1:T(8,128)S(1)} %get-tuple-element.17), channel_id=1, replica_groups=mesh['row_0'=2,'row_1'=4,'col_0'=2,'col_1'=4,'col_2'=2] {'row_1'}, use_global_device_ids=true, to_apply=%region_6.7 | all-reduce | flops 1984 | bytes 15872 | tf_op jit(solution)/shard_map/psum | solution.py:32
  91.0 5.2 %all-reduce.3 = (f32[8,40]{1,0:T(8,128)S(1)}, f32[40,40]{1,0:T(8,128)S(1)}, f32[8,8]{0,1:T(8,128)S(1)}) all-reduce(f32[8,40]{1,0:T(8,128)S(1)} %get-tuple-element.6, f32[40,40]{1,0:T(8,128)S(1)} %get-tuple-element.7, f32[8,8]{0,1:T(8,128)S(1)} %get-tuple-element.8), channel_id=1, replica_groups=mesh['row_0'=2,'row_1'=4,'col_0'=2,'col_1'=4,'col_2'=2] {'col_0'}, use_global_device_ids=true, to_apply=%region_7.8 | all-reduce | flops 1984 | bytes 15872 | tf_op jit(solution)/shard_map/psum | solution.py:32
  96.2 12.6 %all-reduce = (f32[8,40]{1,0:T(8,128)S(1)}, f32[40,40]{1,0:T(8,128)S(1)}, f32[8,8]{0,1:T(8,128)S(1)}) all-reduce(f32[8,40]{1,0:T(8,128)S(1)} %get-tuple-element.12, f32[40,40]{1,0:T(8,128)S(1)} %get-tuple-element.13, f32[8,8]{0,1:T(8,128)S(1)} %get-tuple-element.14), channel_id=1, replica_groups=mesh['row_0'=2,'row_1'=4,'col_0'=2,'col_1'=4,'col_2'=2] {'col_1'}, use_global_device_ids=true, to_apply=%region_8.9 | all-reduce | flops 1984 | bytes 15872 | tf_op jit(solution)/shard_map/psum | solution.py:32
  108.8 14.3 %all-reduce.2 = (f32[8,40]{1,0:T(8,128)S(1)}, f32[40,40]{1,0:T(8,128)S(1)}, f32[8,8]{0,1:T(8,128)S(1)}) all-reduce(f32[8,40]{1,0:T(8,128)S(1)} %get-tuple-element.3, f32[40,40]{1,0:T(8,128)S(1)} %get-tuple-element.4, f32[8,8]{0,1:T(8,128)S(1)} %get-tuple-element.5), channel_id=1, replica_groups=mesh['row_0'=2,'row_1'=4,'col_0'=2,'col_1'=4,'col_2'=2] {'col_2'}, use_global_device_ids=true, to_apply=%region_9.10 | all-reduce | flops 1984 | bytes 15872 | tf_op jit(solution)/shard_map/psum | solution.py:32
  123.1 0.1 fusion.12
  123.3 0.3 fusion.2
  123.9 0.1 fusion.13
  124.1 0.7 cholesky.16
  124.9 0.6 compare_reduce_fusion
  125.6 1.2 select_bitcast_fusion
  126.8 0.6 custom-call.6
  127.4 1.0 fusion.23
  (20 shorter events, 0.8 us)
Async XLA Ops:
  0.6 1.0 copy-start
  3.9 7.6 %copy-start.2 = (s32[192]{0:T(256)S(1)}, s32[192]{0:T(256)}, u32[]{:S(2)}) copy-start(s32[192]{0:T(256)} %param.8) | copy-start | bytes 2308
  4.0 8.3 %copy-start.3 = (s32[192]{0:T(256)S(1)}, s32[192]{0:T(256)}, u32[]{:S(2)}) copy-start(s32[192]{0:T(256)} %param.9) | copy-start | bytes 2308
  4.0 28.1 %all-to-all-start = ((bf16[8,3,8,4096]{3,2,1,0:T(8,128)(2,1)}), bf16[8,3,8,4096]{3,2,1,0:T(8,128)(2,1)S(1)}, u32[]{:S(2)}, u32[]{:S(2)}) async-start(bf16[8,3,8,4096]{3,2,1,0:T(8,128)(2,1)} %broadcast_in_dim.20), calls=%async_computation | async-start | bytes 3145728 | tf_op jit(solution)/shard_map/all_to_all | solution.py:16
  32.1 21.6 %all-to-all-start.2 = ((s32[1,16,12]{2,0,1:T(1,128)}), s32[1,16,12]{2,0,1:T(1,128)S(1)}, u32[]{:S(2)}, u32[]{:S(2)}) async-start(s32[1,16,12]{2,0,1:T(1,128)} %bitcast.7), calls=%async_computation.2 | async-start | bytes 16384 | tf_op jit(solution)/shard_map/all_to_all | solution.py:60
  53.6 14.0 %all-to-all-start.1 = ((bf16[8,16,1536]{2,0,1:T(8,128)(2,1)}), bf16[8,16,1536]{2,0,1:T(8,128)(2,1)S(1)}, u32[]{:S(2)}, u32[]{:S(2)}) async-start(bf16[8,16,1536]{2,0,1:T(8,128)(2,1)} %bitcast.6), calls=%async_computation.1 | async-start | bytes 786432 | tf_op jit(solution)/shard_map/all_to_all | solution.py:57
  123.3 5.1 %copy-start.1 = (f32[8,40]{1,0:T(8,128)}, f32[8,40]{1,0:T(8,128)S(1)}, u32[]{:S(2)}) copy-start(f32[8,40]{1,0:T(8,128)S(1)} %fusion.12) | copy-start | bytes 3844
where the time goes:
time: 129 us; the launch traced here: 128 us
  blocking collectives  53.9 us (42%)
  waiting for transfers between devices  27.7 us (21%)
  starting transfers between devices  19.9 us (15%)
  matrix products  15.3 us (12%)
  local copies, waits for them, and re-layouts  7.52 us (6%)
  other arithmetic  3.33 us (3%)
    psum x5, blocking collectives, by_axis(): value = lax.psum(value, axis)  53.9 us
    all_to_all x1, waiting for transfers between devices, from_everyone(): return lax.all_to_all(copies, axis, split_axis=0, concat_axis=0, tiled=True)  19.8 us
    dot_general x1, matrix products, shards(): jnp.einsum('mtij,mbtj->bti', tiles, picked, preferred_element_type=jnp.fl...  11.3 us
    all_to_all x1, waiting for transfers between devices, shards(): lax.all_to_all(outgoing.astype(jnp.bfloat16), COL, split_axis=1, concat_a...  7.9 us
    all_to_all x1, starting transfers between devices, from_everyone(): return lax.all_to_all(copies, axis, split_axis=0, concat_axis=0, tiled=True)  7.6 us
    all_to_all x1, starting transfers between devices, shards(): lax.all_to_all(row_ids, COL, split_axis=1, concat_axis=1, tiled=True)  6.57 us
    all_to_all x1, starting transfers between devices, shards(): lax.all_to_all(outgoing.astype(jnp.bfloat16), COL, split_axis=1, concat_a...  5.72 us
  transfers between devices with their start and end apart: 3, of which 2 were waited for; matrix products, arithmetic and copies ran while one was open for 12% of the time, Pallas kernels for 0%

commit v1 on v0

v1 whole, which is shorter than its diff:
```python
import functools
import math

import jax
import jax.numpy as jnp
from jax import lax
from jax.experimental import pallas as pl
from jax.experimental.pallas import tpu as pltpu
from jax.sharding import Mesh
from jax.sharding import PartitionSpec as P

AXES = ("xh", "y", "xl", "z", "core")
SIZES = (2, 4, 2, 4, 2)
MESH = pl.DeviceIdType.MESH
F32, BF16 = jnp.float32, jnp.bfloat16
NT = (((1,), (1,)), ((), ()))

COLS, ROWS = 16, 8
MATS, BS, KD, TILE = 3, 8, 40, 128
REGION = 32
PER = 12
SLOTS = 16
KP = 48
STACK = 80


def split3(value):
    high = value.astype(BF16).astype(F32)
    rest = value - high
    middle = rest.astype(BF16).astype(F32)
    return high, middle, rest - middle


def step_kernel(
    basis_hbm, expand_hbm, rows_hbm, cols_hbm, tiles, st, total, pq,
    basis, expand, rows, cols, a_vm, xb, xf, acc, ysend, yrecv, rf, app, onehot, ids_s, ids_r, c1, c2, m1, m2, cw,
    in_sem, tile_sem, g_send, g_recv, i_send, i_recv, c1_send, c1_recv, c2_send, c2_recv,
    y_send, y_recv, m1_send, m1_recv, m2_send, m2_recv,
):
    xh, y, xl, z, core = (lax.axis_index(a) for a in AXES)
    row, col = xh * 4 + y, xl * 8 + z * 2 + core

    def col_peer(j):
        px, pz, pk = lax.rem(xl + j // 8, 2), lax.rem(z + (j // 2) % 4, 4), lax.rem(core + j % 2, 2)
        return (xh, y, px, pz, pk), px * 8 + pz * 2 + pk

    def col_source(j):
        px, pz, pk = lax.rem(xl + j // 8, 2), lax.rem(z + 4 - (j // 2) % 4, 4), lax.rem(core + j % 2, 2)
        return px * 8 + pz * 2 + pk

    def row_peer(j):
        ph, py = lax.rem(xh + j // 4, 2), lax.rem(y + j % 4, 4)
        return (ph, py, xl, z, core)

    def remote(src, dst, send, recv, device):
        return pltpu.make_async_remote_copy(
            src_ref=src, dst_ref=dst, send_sem=send, recv_sem=recv, device_id=device, device_id_type=MESH
        )

    barrier = pltpu.get_barrier_semaphore()
    for j in range(1, ROWS):
        pl.semaphore_signal(barrier, inc=1, device_id=row_peer(j), device_id_type=MESH)
    for j in range(1, COLS):
        pl.semaphore_signal(barrier, inc=1, device_id=col_peer(j)[0], device_id_type=MESH)

    in_copies = [
        pltpu.make_async_copy(src, dst, in_sem.at[i])
        for i, (src, dst) in enumerate(
            ((basis_hbm, basis), (expand_hbm, expand), (rows_hbm, rows), (cols_hbm, cols))
        )
    ]
    for copy in in_copies:
        copy.start()
    tile_copies = []
    for m in range(MATS):
        for q in range(4):
            part = pl.ds(48 * q, 48)
            copy = pltpu.make_async_copy(tiles.at[m, part], a_vm.at[m, part], tile_sem.at[m, q])
            copy.start()
            tile_copies.append(copy)

    in_copies[0].wait()
    in_copies[1].wait()
    coef = jnp.concatenate([expand[m] for m in range(MATS)], axis=0)
    lhs = jnp.concatenate(split3(coef), axis=0).astype(BF16)
    for n in range(8):
        wide = jnp.dot(lhs, basis[:, n * 512 : (n + 1) * 512], preferred_element_type=F32)
        for m in range(MATS):
            a, b, c = (wide[24 * i + 8 * m : 24 * i + 8 * m + 8] for i in range(3))
            value = (c + b) + a
            for h in range(2):
                pair = jnp.concatenate(
                    [value[:, (2 * h + i) * TILE : (2 * h + i + 1) * TILE] for i in range(2)], axis=0
                )
                xb[row, m, 64 * (n // 2) + 32 * (n % 2) + 16 * h : 64 * (n // 2) + 32 * (n % 2) + 16 * h + 16, :] = pair.astype(BF16)

    pl.semaphore_wait(barrier, ROWS + COLS - 2)

    up, down = lax.rem(y + 1, 4), lax.rem(y + 3, 4)
    far, other = lax.rem(y + 2, 4), 1 - xh
    to_up, to_down, to_other = (xh, up, xl, z, core), (xh, down, xl, z, core), (other, y, xl, z, core)
    whole, first, second = pl.ds(0, 256), pl.ds(0, 128), pl.ds(128, 128)

    def gather(m, i, slot, part, device):
        ref = xb.at[slot, m, part]
        return remote(ref, ref, g_send.at[m, i], g_recv.at[m, i], device)

    def moves(m):
        return (
            gather(m, 0, row, whole, to_up),
            gather(m, 1, row, whole, to_down),
            gather(m, 2, row, whole, to_other),
            gather(m, 3, xh * 4 + down, first, to_up),
            gather(m, 4, xh * 4 + up, second, to_down),
            gather(m, 5, other * 4 + y, whole, to_up),
            gather(m, 6, other * 4 + y, whole, to_down),
            gather(m, 7, xh * 4 + far, first, to_other),
            gather(m, 8, xh * 4 + far, second, to_other),
        )

    hops = [moves(m) for m in range(MATS)]
    for m in range(MATS):
        for i in (2, 0, 1):
            hops[m][i].start()

    in_copies[2].wait()
    in_copies[3].wait()

    def fill_ids(k, carry):
        for u in range(SLOTS):
            if u < PER:
                value = rows[k * PER + u] - k * REGION
            else:
                value = jnp.int32(-1)
            ids_s[k, u : u + 1, :] = jnp.full((1, TILE), value, jnp.int32)
        return carry

    lax.fori_loop(0, COLS, fill_ids, 0)
    id_copies = []
    for j in range(1, COLS):
        device, k = col_peer(j)
        copy = remote(ids_s.at[k], ids_r.at[col], i_send.at[j], i_recv.at[j], device)
        copy.start()
        id_copies.append(copy)
    ids_r[col] = ids_s[col]

    st[0:KD, :] = basis[...]
    st[KD:KP, :] = jnp.zeros((KP - KD, st.shape[1]), BF16)
    own = lax.dot_general(st[0:KP, :], st[0:KP, :], NT, preferred_element_type=F32)
    cw[...] = jnp.zeros(cw.shape, F32)
    cw[:, 0:KP] = own
    packed = cw[0:16, :] + pltpu.roll(cw[16:32, :], 40, 1) + pltpu.roll(cw[32:48, :], 80, 1)
    c1[col] = packed
    c1_copies = []
    for j in range(1, COLS):
        device, _ = col_peer(j)
        copy = remote(c1.at[col], c1.at[col], c1_send.at[j], c1_recv.at[j], device)
        copy.start()
        c1_copies.append(copy)

    def relay(m):
        h = hops[m]
        h[0].wait_recv()
        h[3].start()
        h[1].wait_recv()
        h[4].start()
        h[2].wait_recv()
        h[5].start()
        h[6].start()
        h[3].wait_recv()
        h[7].start()
        h[4].wait_recv()
        h[8].start()

    def arrive(m):
        for i in (5, 6, 7, 8):
            hops[m][i].wait_recv()
        for r in range(ROWS):
            xf[r * REGION : (r + 1) * REGION] = xb[r, m].astype(F32).reshape(REGION, BS, TILE)
        for q in range(4):
            tile_copies[4 * m + q].wait()

    zero = jnp.zeros((BS, TILE), F32)

    def pair_product(m, t):
        x0, x1 = xf[cols[t]], xf[cols[t + 1]]
        lhs = jnp.concatenate(
            [jnp.concatenate([x0, zero], axis=1), jnp.concatenate([zero, x1], axis=1)], axis=0
        ).astype(BF16)
        rhs = jnp.concatenate([a_vm[m, t], a_vm[m, t + 1]], axis=1)
        return lax.dot_general(lhs, rhs, NT, preferred_element_type=F32)

    def run_first(k, carry):
        for p in range(PER // 2):
            acc[k, 16 * p : 16 * p + 16, :] = pair_product(0, k * PER + 2 * p)
        return carry

    def run_second(k, carry):
        for p in range(PER // 2):
            acc[k, 16 * p : 16 * p + 16, :] += pair_product(1, k * PER + 2 * p)
        return carry

    def run_last(k):
        for p in range(PER // 2):
            part = slice(16 * p, 16 * p + 16)
            ysend[k, part, :] = (acc[k, part, :] + pair_product(2, k * PER + 2 * p)).astype(BF16)

    relay(0)
    relay(1)
    arrive(0)
    lax.fori_loop(0, COLS, run_first, 0)
    relay(2)

    for copy in c1_copies:
        copy.wait_recv()
    half = c1[0]
    for k in range(1, COLS):
        half = half + c1[k]
    c2[row] = half
    c2_copies = []
    for j in range(1, ROWS):
        copy = remote(c2.at[row], c2.at[row], c2_send.at[j], c2_recv.at[j], row_peer(j))
        copy.start()
        c2_copies.append(copy)

    for copy in id_copies:
        copy.wait_recv()
    lane = lax.broadcasted_iota(jnp.int32, (COLS * SLOTS, TILE), 1)
    chosen = jnp.where(ids_r[...].reshape(COLS * SLOTS, TILE) == lane, 1.0, 0.0).astype(F32)
    onehot[...] = chosen.T[0:REGION, :].astype(BF16)
    for k in range(COLS):
        rf[k, PER * BS :, :] = jnp.zeros(((SLOTS - PER) * BS, TILE), F32)

    arrive(1)
    lax.fori_loop(0, COLS, run_second, 0)

    for copy in c2_copies:
        copy.wait_recv()
    full = c2[0]
    for r in range(1, ROWS):
        full = full + c2[r]
    lanes = lax.broadcasted_iota(jnp.int32, (16, TILE), 1)
    keep = lanes < KD
    for i in range(3):
        cw[16 * i : 16 * i + 16, :] = jnp.where(keep, full if i == 0 else pltpu.roll(full, TILE - 40 * i, 1), 0.0)
    entries = float(st.shape[1] * ROWS * COLS)
    corr = cw[:, 0:KP] * (1.0 / entries)
    eye = jnp.where(
        lax.broadcasted_iota(jnp.int32, (KP, KP), 0) == lax.broadcasted_iota(jnp.int32, (KP, KP), 1), 1.0, 0.0
    ).astype(F32)
    dot = functools.partial(jnp.dot, precision=lax.Precision.HIGHEST, preferred_element_type=F32)
    corr2 = dot(corr, corr)
    pq[0] = 2.0 * eye - corr
    pq[1] = 4.0 * eye - 6.0 * corr + 4.0 * corr2 - dot(corr2, corr)

    arrive(2)

    def result_copy(j):
        device, k = col_peer(j)
        return remote(ysend.at[k], yrecv.at[col], y_send.at[j], y_recv.at[j], device)

    def last(j, carry):
        run_last(col_peer(j)[1])
        result_copy(j).start()
        return carry

    lax.fori_loop(1, COLS, last, 0)
    run_last(col)
    rf[col, 0 : PER * BS, :] = ysend[col].astype(F32)

    def landed(j, carry):
        k = col_source(j)
        result_copy(j).wait_recv()
        rf[k, 0 : PER * BS, :] = yrecv[k].astype(F32)
        return carry

    lax.fori_loop(1, COLS, landed, 0)

    for b in range(0, BS, 2):
        pair = [
            jnp.concatenate([rf[k, pl.ds(b + i, SLOTS, stride=BS), :] for k in range(COLS)], axis=0) for i in range(2)
        ]
        both = jnp.dot(onehot[...], jnp.concatenate(pair, axis=1).astype(BF16), preferred_element_type=F32)
        for i in range(2):
            app[pl.ds(b + i, REGION, stride=BS), :] = both[:, i * TILE : (i + 1) * TILE]
    for s in range(REGION):
        parts = split3(app[s * BS : (s + 1) * BS, :])
        st[KP:STACK, s * TILE : (s + 1) * TILE] = jnp.concatenate([*parts, zero], axis=0).astype(BF16)

    inner = lax.dot_general(st[KP:STACK, :], st[...], NT, preferred_element_type=F32)
    m1[col, :, 0:STACK] = (inner[16:24] + inner[8:16]) + inner[0:8]
    m1[col, :, STACK:] = jnp.zeros((BS, TILE - STACK), F32)
    m1_copies = []
    for j in range(1, COLS):
        device, _ = col_peer(j)
        copy = remote(m1.at[col], m1.at[col], m1_send.at[j], m1_recv.at[j], device)
        copy.start()
        m1_copies.append(copy)
    for copy in m1_copies:
        copy.wait_recv()
    half = m1[0]
    for k in range(1, COLS):
        half = half + m1[k]
    m2[row] = half
    m2_copies = []
    for j in range(1, ROWS):
        copy = remote(m2.at[row], m2.at[row], m2_send.at[j], m2_recv.at[j], row_peer(j))
        copy.start()
        m2_copies.append(copy)
    for copy in m2_copies:
        copy.wait_recv()
    full = m2[0]
    for r in range(1, ROWS):
        full = full + m2[r]
    total[...] = full

    for m in range(MATS):
        for copy in hops[m]:
            copy.wait_send()
    for copy in (*id_copies, *c1_copies, *c2_copies, *m1_copies, *m2_copies):
        copy.wait_send()

    def sent(j, carry):
        result_copy(j).wait_send()
        return carry

    lax.fori_loop(1, COLS, sent, 0)


def final_kernel(st, total, pq, new_block, coefficients, factor, *, entries):
    inverse_root = 1.0 / math.sqrt(entries)
    dot = functools.partial(lax.dot_general, precision=lax.Precision.HIGHEST, preferred_element_type=F32)
    nn = (((1,), (0,)), ((), ()))
    tot = total[...]
    raw = tot[:, 0:KP] * inverse_root
    energy = (
        pltpu.roll(tot, TILE - KP, 1) + pltpu.roll(tot, TILE - KP - 8, 1) + pltpu.roll(tot, TILE - KP - 16, 1)
    )[:, 0:BS]
    coef = dot(raw, pq[0], nn)
    gram = (energy - dot(dot(raw, pq[1], nn), raw, NT)) * (1.0 / entries)
    coefficients[...] = coef[:, 0:KD]

    sub = lax.broadcasted_iota(jnp.int32, (BS, TILE), 0)
    lane = lax.broadcasted_iota(jnp.int32, (BS, TILE), 1)
    unit = (lane == sub + KP) | (lane == sub + KP + 8) | (lane == sub + KP + 16)
    target = jnp.where(unit, 1.0, 0.0).astype(F32)
    target = target + jnp.concatenate([coef * -inverse_root, jnp.zeros((BS, TILE - KP), F32)], axis=1)
    left = jnp.concatenate([gram, jnp.zeros((BS, TILE - BS), F32)], axis=1)
    lower = jnp.zeros((BS, TILE), F32)
    for j in range(BS):
        root = jnp.sqrt(left[j : j + 1, j : j + 1])
        scale = jnp.broadcast_to(1.0 / root, (BS, 1))
        column = jnp.broadcast_to(left[:, j : j + 1] * scale, (BS, TILE))
        below = jnp.where(sub > j, column, 0.0)
        lower = jnp.where((lane == j) & (sub >= j), column, lower)
        solved = jnp.broadcast_to(target[j : j + 1, :], (BS, TILE)) * scale
        target = jnp.where(sub == j, solved, target - below * solved)
        left = left - below * (jnp.broadcast_to(left[j : j + 1, :], (BS, TILE)) * scale)
    factor[...] = lower[:, 0:BS]
    mix = jnp.concatenate(split3(target[:, 0:STACK]), axis=0).astype(BF16)
    length = st.shape[1]
    for n in range(length // 512):
        part = slice(n * 512, (n + 1) * 512)
        wide = jnp.dot(mix, st[:, part], preferred_element_type=F32)
        new_block[:, part] = (wide[16:24] + wide[8:16]) + wide[0:8]


def shards(basis, expand, tiles, tile_rows, tile_cols):
    length = basis.shape[1]
    vmem = pl.BlockSpec(memory_space=pltpu.VMEM)
    hbm = pl.BlockSpec(memory_space=pltpu.HBM)
    dma = pltpu.SemaphoreType.DMA
    st, total, pq = pl.pallas_call(
        step_kernel,
        out_shape=(
            jax.ShapeDtypeStruct((STACK, length), BF16),
            jax.ShapeDtypeStruct((BS, TILE), F32),
            jax.ShapeDtypeStruct((2, KP, KP), F32),
        ),
        in_specs=[hbm] * 5,
        out_specs=(vmem, vmem, vmem),
        scratch_shapes=[
            pltpu.VMEM(basis.shape, BF16),
            pltpu.VMEM(expand.shape, F32),
            pltpu.SMEM(tile_rows.shape, jnp.int32),
            pltpu.SMEM(tile_cols.shape, jnp.int32),
            pltpu.VMEM(tiles.shape, BF16),
            pltpu.VMEM((ROWS, MATS, 256, TILE), BF16),
            pltpu.VMEM((ROWS * REGION, BS, TILE), F32),
            pltpu.VMEM((COLS, PER * BS, TILE), F32),
            pltpu.VMEM((COLS, PER * BS, TILE), BF16),
            pltpu.VMEM((COLS, PER * BS, TILE), BF16),
            pltpu.VMEM((COLS, SLOTS * BS, TILE), F32),
            pltpu.VMEM((REGION * BS, TILE), F32),
            pltpu.VMEM((REGION, COLS * SLOTS), BF16),
            pltpu.VMEM((COLS, SLOTS, TILE), jnp.int32),
            pltpu.VMEM((COLS, SLOTS, TILE), jnp.int32),
            pltpu.VMEM((COLS, 16, TILE), F32),
            pltpu.VMEM((ROWS, 16, TILE), F32),
            pltpu.VMEM((COLS, BS, TILE), F32),
            pltpu.VMEM((ROWS, BS, TILE), F32),
            pltpu.VMEM((KP, TILE), F32),
            dma((4,)),
            dma((MATS, 4)),
            dma((MATS, 9)), dma((MATS, 9)),
            dma((COLS,)), dma((COLS,)),
            dma((COLS,)), dma((COLS,)),
            dma((ROWS,)), dma((ROWS,)),
            dma((COLS,)), dma((COLS,)),
            dma((COLS,)), dma((COLS,)),
            dma((ROWS,)), dma((ROWS,)),
        ],
        compiler_params=pltpu.CompilerParams(
            collective_id=0, has_side_effects=True, vmem_limit_bytes=36 * 2**20
        ),
        name="toar_step",
    )(basis, expand, tile_rows, tile_cols, tiles)
    return tuple(
        pl.pallas_call(
            functools.partial(final_kernel, entries=length * ROWS * COLS),
            out_shape=(
                jax.ShapeDtypeStruct((BS, length), F32),
                jax.ShapeDtypeStruct((BS, KD), F32),
                jax.ShapeDtypeStruct((BS, BS), F32),
            ),
            in_specs=[vmem, vmem, vmem],
            out_specs=(vmem, vmem, vmem),
            compiler_params=pltpu.CompilerParams(vmem_limit_bytes=8 * 2**20),
            name="toar_final",
        )(st, total, pq)
    )


def solution(mesh):
    finer = Mesh(mesh.devices.reshape(SIZES), AXES)
    return jax.shard_map(
        shards,
        mesh=finer,
        in_specs=(P(None, AXES), P(), P(None, AXES, None, None), P(AXES), P(AXES)),
        out_specs=(P(None, AXES), P(), P()),
        check_vma=False,
    )
```

time: 129 us -> 57.8 us (0.45)
  Pallas kernels: 0 us -> 53.9 us
  blocking collectives: 53.9 us -> 0 us
  waiting for transfers between devices: 27.7 us -> 0 us
  starting transfers between devices: 19.9 us -> 0 us
  matrix products: 15.3 us -> 0 us
  local copies, waits for them, and re-layouts: 7.52 us -> 3.03 us
  other arithmetic: 3.33 us -> 0 us
    psum x5 -> x0, blocking collectives: 53.9 us -> none  [by_axis(): value = lax.psum(value, axis)]
    pallas_call x0 -> x2, Pallas kernels: none -> 53.9 us  [the longest x1 51.8 us: shards(): pl.pallas_call(step_kernel, out_shape=(jax.ShapeDtypeStruct((STACK, lengt...]
    all_to_all x3 -> x0, waiting for transfers between devices: 27.7 us -> none  [the longest x1 19.8 us: from_everyone(): return lax.all_to_all(copies, axis, split_axis=0, concat_axis=0, tiled=True)]
    all_to_all x3 -> x0, starting transfers between devices: 19.9 us -> none  [the longest x1 7.6 us: from_everyone(): return lax.all_to_all(copies, axis, split_axis=0, concat_axis=0, tiled=True)]
    dot_general x11 -> x0, matrix products: 14.3 us -> none  [the longest x1 11.3 us: shards(): jnp.einsum('mtij,mbtj->bti', tiles, picked, preferred_element_type=jnp.fl...]
    another operation x5 -> x0, other arithmetic: 3.27 us -> none  [the longest x2 1.86 us: shards(): lax.linalg.triangular_solve(factor, cleaned, left_side=True, lower=True)]
    unnamed x8, local copies, waits for them, and re-layouts: 0.98 us -> 3.03 us
    another operation x2 -> x0, local copies, waits for them, and re-layouts: 1.8 us -> none  [shards(): gathered.reshape(3, block_size, row_count * length // tile_size, tile_size)]
  transfers between devices with their start and end apart: 3 -> 0, of which waited for: 2 -> 0; matrix products, arithmetic and copies ran while one was open for 12% -> 0% of each run, Pallas kernels for 0% -> 0%
where the time goes in v1:
time: 57.8 us; the launch traced here: 57.6 us
  Pallas kernels  53.9 us (93%)
  local copies, waits for them, and re-layouts  3.03 us (5%)
  between operations  0.65 us (1%)
    pallas_call x1, Pallas kernels, shards(): pl.pallas_call(step_kernel, out_shape=(jax.ShapeDtypeStruct((STACK, lengt...  51.8 us
    unnamed x8, local copies, waits for them, and re-layouts  3.03 us
    pallas_call x1, Pallas kernels, shards(): pl.pallas_call(functools.partial(final_kernel, entries=length * ROWS * CO...  2.11 us

profile of v1, /device:TPU:1, one launch (start us, length us, event | category | flops | bytes accessed | tf_op | source)
XLA Modules:
  0.0 57.6 jit_solution(14231107438749823828)
XLA Ops:
  0.6 0.0 copy-start
  0.6 1.0 %copy-done = bf16[40,4096]{1,0:T(8,128)(2,1)S(1)} copy-done((bf16[40,4096]{1,0:T(8,128)(2,1)S(1)}, bf16[40,4096]{1,0:T(8,128)(2,1)}, u32[]{:S(2)}) %copy-start) | copy-done | bytes 327704
  1.6 0.0 copy-start.1
  1.6 0.7 %copy-done.1 = f32[3,8,40]{2,1,0:T(8,128)S(1)} copy-done((f32[3,8,40]{2,1,0:T(8,128)S(1)}, f32[3,8,40]{2,1,0:T(8,128)}, u32[]{:S(2)}) %copy-start.1) | copy-done | bytes 3864
  2.3 0.0 copy-start.2
  2.3 0.7 %copy-done.2 = s32[192]{0:T(256)S(1)} copy-done((s32[192]{0:T(256)S(1)}, s32[192]{0:T(256)}, u32[]{:S(2)}) %copy-start.2) | copy-done | bytes 792
  3.0 0.0 copy-start.3
  3.0 0.7 %copy-done.3 = s32[192]{0:T(256)S(1)} copy-done((s32[192]{0:T(256)S(1)}, s32[192]{0:T(256)}, u32[]{:S(2)}) %copy-start.3) | copy-done | bytes 792
  3.7 51.8 %toar_step.1 = (bf16[80,4096]{1,0:T(8,128)(2,1)S(1)}, f32[8,128]{1,0:T(8,128)S(1)}, f32[2,48,48]{2,1,0:T(8,128)S(1)}) custom-call(bf16[40,4096]{1,0:T(8,128)(2,1)S(1)} %copy-done, f32[3,8,40]{2,1,0:T(8,128)S(1)} %copy-done.1, s32[192]{0:T(256)S(1)} %copy-done.2, s32[192]{0:T(256)S(1)} %copy-done.3, bf16[3,192,128,128]{3,2,1,0:T(8,128)(2,1)} %tiles.1), custom_call_target="tpu_custom_call" | custom-call | tf_op jit(solution)/shard_map/toar_step/pallas_call | solution.py:373
  55.5 2.1 %toar_final.1 = (f32[8,4096]{1,0:T(8,128)}, f32[8,40]{1,0:T(8,128)}, f32[8,8]{1,0:T(8,128)}) custom-call(bf16[80,4096]{1,0:T(8,128)(2,1)S(1)} %get-tuple-element.6.st, f32[8,128]{1,0:T(8,128)S(1)} %get-tuple-element.7.total, f32[2,48,48]{2,1,0:T(8,128)S(1)} %get-tuple-element.8.pq), custom_call_target="tpu_custom_call" | custom-call | tf_op jit(solution)/shard_map/toar_final/pallas_call | solution.py:419
Async XLA Ops:
  0.6 1.0 %copy-start = (bf16[40,4096]{1,0:T(8,128)(2,1)S(1)}, bf16[40,4096]{1,0:T(8,128)(2,1)}, u32[]{:S(2)}) copy-start(bf16[40,4096]{1,0:T(8,128)(2,1)} %basis_hbm.1) | copy-start | bytes 983044
  1.6 0.7 %copy-start.1 = (f32[3,8,40]{2,1,0:T(8,128)S(1)}, f32[3,8,40]{2,1,0:T(8,128)}, u32[]{:S(2)}) copy-start(f32[3,8,40]{2,1,0:T(8,128)} %expand_hbm.1) | copy-start | bytes 11524
  2.3 0.7 %copy-start.2 = (s32[192]{0:T(256)S(1)}, s32[192]{0:T(256)}, u32[]{:S(2)}) copy-start(s32[192]{0:T(256)} %rows_hbm.1) | copy-start | bytes 2308
  3.0 0.7 %copy-start.3 = (s32[192]{0:T(256)S(1)}, s32[192]{0:T(256)}, u32[]{:S(2)}) copy-start(s32[192]{0:T(256)} %cols_hbm.1) | copy-start | bytes 2308

commit v2 on v1

--- a/solution.py
+++ b/solution.py
@@ -71,6 +71,8 @@
     ]
     for copy in in_copies:
         copy.start()
+    in_copies[0].wait()
+    in_copies[1].wait()
     tile_copies = []
     for m in range(MATS):
         for q in range(4):
@@ -79,8 +81,6 @@
             copy.start()
             tile_copies.append(copy)
 
-    in_copies[0].wait()
-    in_copies[1].wait()
     coef = jnp.concatenate([expand[m] for m in range(MATS)], axis=0)
     lhs = jnp.concatenate(split3(coef), axis=0).astype(BF16)
     for n in range(8):
@@ -158,20 +158,6 @@
         copy.start()
         c1_copies.append(copy)
 
-    def relay(m):
-        h = hops[m]
-        h[0].wait_recv()
-        h[3].start()
-        h[1].wait_recv()
-        h[4].start()
-        h[2].wait_recv()
-        h[5].start()
-        h[6].start()
-        h[3].wait_recv()
-        h[7].start()
-        h[4].wait_recv()
-        h[8].start()
-
     def arrive(m):
         for i in (5, 6, 7, 8):
             hops[m][i].wait_recv()
@@ -205,11 +191,47 @@
             part = slice(16 * p, 16 * p + 16)
             ysend[k, part, :] = (acc[k, part, :] + pair_product(2, k * PER + 2 * p)).astype(BF16)
 
-    relay(0)
-    relay(1)
+    for h in hops:
+        h[0].wait_recv()
+        h[3].start()
+        h[1].wait_recv()
+        h[4].start()
+    for h in hops:
+        h[2].wait_recv()
+        h[5].start()
+        h[6].start()
+    for h in hops:
+        h[3].wait_recv()
+        h[7].start()
+        h[4].wait_recv()
+        h[8].start()
+
+    for copy in id_copies:
+        copy.wait_recv()
+    lane = lax.broadcasted_iota(jnp.int32, (COLS * SLOTS, TILE), 1)
+    chosen = jnp.where(ids_r[...].reshape(COLS * SLOTS, TILE) == lane, 1.0, 0.0).astype(F32)
+    onehot[...] = chosen.T[0:REGION, :].astype(BF16)
+    for k in range(COLS):
+        rf[k, PER * BS :, :] = jnp.zeros(((SLOTS - PER) * BS, TILE), F32)
+
     arrive(0)
-    lax.fori_loop(0, COLS, run_first, 0)
-    relay(2)
+    lax.fori_loop(0, COLS, run_first, 0, unroll=COLS)
+    arrive(1)
+    lax.fori_loop(0, COLS, run_second, 0, unroll=COLS)
+
+    arrive(2)
+
+    def result_copy(j):
+        device, k = col_peer(j)
+        return remote(ysend.at[k], yrecv.at[col], y_send.at[j], y_recv.at[j], device)
+
+    def last(j, carry):
+        run_last(col_peer(j)[1])
+        result_copy(j).start()
+        return carry
+
+    lax.fori_loop(1, COLS, last, 0, unroll=COLS - 1)
+    run_last(col)
 
     for copy in c1_copies:
         copy.wait_recv()
@@ -223,17 +245,36 @@
         copy.start()
         c2_copies.append(copy)
 
-    for copy in id_copies:
-        copy.wait_recv()
-    lane = lax.broadcasted_iota(jnp.int32, (COLS * SLOTS, TILE), 1)
-    chosen = jnp.where(ids_r[...].reshape(COLS * SLOTS, TILE) == lane, 1.0, 0.0).astype(F32)
-    onehot[...] = chosen.T[0:REGION, :].astype(BF16)
-    for k in range(COLS):
-        rf[k, PER * BS :, :] = jnp.zeros(((SLOTS - PER) * BS, TILE), F32)
-
-    arrive(1)
-    lax.fori_loop(0, COLS, run_second, 0)
-
+    rf[col, 0 : PER * BS, :] = ysend[col].astype(F32)
+
+    def landed(j, carry):
+        k = col_source(j)
+        result_copy(j).wait_recv()
+        rf[k, 0 : PER * BS, :] = yrecv[k].astype(F32)
+        return carry
+
+    lax.fori_loop(1, COLS, landed, 0, unroll=COLS - 1)
+
+    for b in range(0, BS, 2):
+        pair = [
+            jnp.concatenate([rf[k, pl.ds(b + i, SLOTS, stride=BS), :] for k in range(COLS)], axis=0) for i in range(2)
+        ]
+        both = jnp.dot(onehot[...], jnp.concatenate(pair, axis=1).astype(BF16), preferred_element_type=F32)
+        for i in range(2):
+            app[pl.ds(b + i, REGION, stride=BS), :] = both[:, i * TILE : (i + 1) * TILE]
+    for s in range(REGION):
+        parts = split3(app[s * BS : (s + 1) * BS, :])
+        st[KP:STACK, s * TILE : (s + 1) * TILE] = jnp.concatenate([*parts, zero], axis=0).astype(BF16)
+
+    inner = lax.dot_general(st[KP:STACK, :], st[...], NT, preferred_element_type=F32)
+    m1[col, :, 0:STACK] = (inner[16:24] + inner[8:16]) + inner[0:8]
+    m1[col, :, STACK:] = jnp.zeros((BS, TILE - STACK), F32)
+    m1_copies = []
+    for j in range(1, COLS):
+        device, _ = col_peer(j)
+        copy = remote(m1.at[col], m1.at[col], m1_send.at[j], m1_recv.at[j], device)
+        copy.start()
+        m1_copies.append(copy)
     for copy in c2_copies:
         copy.wait_recv()
     full = c2[0]
@@ -253,49 +294,6 @@
     pq[0] = 2.0 * eye - corr
     pq[1] = 4.0 * eye - 6.0 * corr + 4.0 * corr2 - dot(corr2, corr)
 
-    arrive(2)
-
-    def result_copy(j):
-        device, k = col_peer(j)
-        return remote(ysend.at[k], yrecv.at[col], y_send.at[j], y_recv.at[j], device)
-
-    def last(j, carry):
-        run_last(col_peer(j)[1])
-        result_copy(j).start()
-        return carry
-
-    lax.fori_loop(1, COLS, last, 0)
-    run_last(col)
-    rf[col, 0 : PER * BS, :] = ysend[col].astype(F32)
-
-    def landed(j, carry):
-        k = col_source(j)
-        result_copy(j).wait_recv()
-        rf[k, 0 : PER * BS, :] = yrecv[k].astype(F32)
-        return carry
-
-    lax.fori_loop(1, COLS, landed, 0)
-
-    for b in range(0, BS, 2):
-        pair = [
-            jnp.concatenate([rf[k, pl.ds(b + i, SLOTS, stride=BS), :] for k in range(COLS)], axis=0) for i in range(2)
-        ]
-        both = jnp.dot(onehot[...], jnp.concatenate(pair, axis=1).astype(BF16), preferred_element_type=F32)
-        for i in range(2):
-            app[pl.ds(b + i, REGION, stride=BS), :] = both[:, i * TILE : (i + 1) * TILE]
-    for s in range(REGION):
-        parts = split3(app[s * BS : (s + 1) * BS, :])
-        st[KP:STACK, s * TILE : (s + 1) * TILE] = jnp.concatenate([*parts, zero], axis=0).astype(BF16)
-
-    inner = lax.dot_general(st[KP:STACK, :], st[...], NT, preferred_element_type=F32)
-    m1[col, :, 0:STACK] = (inner[16:24] + inner[8:16]) + inner[0:8]
-    m1[col, :, STACK:] = jnp.zeros((BS, TILE - STACK), F32)
-    m1_copies = []
-    for j in range(1, COLS):
-        device, _ = col_peer(j)
-        copy = remote(m1.at[col], m1.at[col], m1_send.at[j], m1_recv.at[j], device)
-        copy.start()
-        m1_copies.append(copy)
     for copy in m1_copies:
         copy.wait_recv()
     half = m1[0]
@@ -414,7 +412,7 @@
             collective_id=0, has_side_effects=True, vmem_limit_bytes=36 * 2**20
         ),
         name="toar_step",
-    )(basis, expand, tile_rows, tile_cols, tiles)
+    )(*(pltpu.with_memory_space_constraint(a, pltpu.HBM) for a in (basis, expand, tile_rows, tile_cols, tiles)))
     return tuple(
         pl.pallas_call(
             functools.partial(final_kernel, entries=length * ROWS * COLS),

time: 57.8 us -> 46.2 us (0.80)
  Pallas kernels: 53.9 us -> 45.4 us
  local copies, waits for them, and re-layouts: 3.03 us -> 0 us
    pallas_call x1, Pallas kernels: 51.8 us -> 43.3 us  [shards(): pl.pallas_call(step_kernel, out_shape=(jax.ShapeDtypeStruct((STACK, lengt...]
    unnamed x8 -> x0, local copies, waits for them, and re-layouts: 3.03 us -> none
where the time goes in v2:
time: 46.2 us; the launch traced here: 46.1 us
  Pallas kernels  45.4 us (98%)
  between operations  0.64 us (1%)
    pallas_call x1, Pallas kernels, shards(): pl.pallas_call(step_kernel, out_shape=(jax.ShapeDtypeStruct((STACK, lengt...  43.3 us
    pallas_call x1, Pallas kernels, shards(): pl.pallas_call(functools.partial(final_kernel, entries=length * ROWS * CO...  2.12 us

profile of v2, /device:TPU:1, one launch (start us, length us, event | category | flops | bytes accessed | tf_op | source)
XLA Modules:
  0.0 46.1 jit_solution(11264690505841971382)
XLA Ops:
  0.6 43.3 %toar_step.1 = (bf16[80,4096]{1,0:T(8,128)(2,1)S(1)}, f32[8,128]{1,0:T(8,128)S(1)}, f32[2,48,48]{2,1,0:T(8,128)S(1)}) custom-call(bf16[40,4096]{1,0:T(8,128)(2,1)} %basis_hbm.1, f32[3,8,40]{2,1,0:T(8,128)} %expand_hbm.1, s32[192]{0:T(256)} %rows_hbm.1, s32[192]{0:T(256)} %cols_hbm.1, bf16[3,192,128,128]{3,2,1,0:T(8,128)(2,1)} %tiles.1), custom_call_target="tpu_custom_call" | custom-call | tf_op jit(solution)/shard_map/toar_step/pallas_call | solution.py:371
  43.9 2.1 %toar_final.1 = (f32[8,4096]{1,0:T(8,128)}, f32[8,40]{1,0:T(8,128)}, f32[8,8]{1,0:T(8,128)}) custom-call(bf16[80,4096]{1,0:T(8,128)(2,1)S(1)} %get-tuple-element.6.st, f32[8,128]{1,0:T(8,128)S(1)} %get-tuple-element.7.total, f32[2,48,48]{2,1,0:T(8,128)S(1)} %get-tuple-element.8.pq), custom_call_target="tpu_custom_call" | custom-call | tf_op jit(solution)/shard_map/toar_final/pallas_call | solution.py:417

commit v3 on v2

--- a/solution.py
+++ b/solution.py
@@ -21,6 +21,8 @@
 PER = 12
 SLOTS = 16
 KP = 48
+COL_ORDER = (12, 13, 4, 5, 10, 11, 14, 15, 2, 3, 6, 7, 8, 9, 1)
+ROW_ORDER = (6, 5, 7, 4, 2, 1, 3)
 STACK = 80
 
 
@@ -57,12 +59,6 @@
             src_ref=src, dst_ref=dst, send_sem=send, recv_sem=recv, device_id=device, device_id_type=MESH
         )
 
-    barrier = pltpu.get_barrier_semaphore()
-    for j in range(1, ROWS):
-        pl.semaphore_signal(barrier, inc=1, device_id=row_peer(j), device_id_type=MESH)
-    for j in range(1, COLS):
-        pl.semaphore_signal(barrier, inc=1, device_id=col_peer(j)[0], device_id_type=MESH)
-
     in_copies = [
         pltpu.make_async_copy(src, dst, in_sem.at[i])
         for i, (src, dst) in enumerate(
@@ -71,12 +67,18 @@
     ]
     for copy in in_copies:
         copy.start()
+    barrier = pltpu.get_barrier_semaphore()
+    for j in range(1, ROWS):
+        pl.semaphore_signal(barrier, inc=1, device_id=row_peer(j), device_id_type=MESH)
+    for j in range(1, COLS):
+        pl.semaphore_signal(barrier, inc=1, device_id=col_peer(j)[0], device_id_type=MESH)
+
     in_copies[0].wait()
     in_copies[1].wait()
     tile_copies = []
     for m in range(MATS):
-        for q in range(4):
-            part = pl.ds(48 * q, 48)
+        for q in range(3):
+            part = pl.ds(64 * q, 64)
             copy = pltpu.make_async_copy(tiles.at[m, part], a_vm.at[m, part], tile_sem.at[m, q])
             copy.start()
             tile_copies.append(copy)
@@ -159,17 +161,30 @@
         c1_copies.append(copy)
 
     def arrive(m):
-        for i in (5, 6, 7, 8):
-            hops[m][i].wait_recv()
-        for r in range(ROWS):
-            xf[r * REGION : (r + 1) * REGION] = xb[r, m].astype(F32).reshape(REGION, BS, TILE)
-        for q in range(4):
-            tile_copies[4 * m + q].wait()
+        hops[m][5].wait_recv()
+        unpack(m, other * 4 + down)
+        hops[m][6].wait_recv()
+        unpack(m, other * 4 + up)
+        hops[m][7].wait_recv()
+        hops[m][8].wait_recv()
+        unpack(m, other * 4 + far)
 
     zero = jnp.zeros((BS, TILE), F32)
 
+    def products(m, t):
+        rows_of = []
+        for i in (t, t + 2):
+            x0, x1 = xf[m, cols[i]], xf[m, cols[i + 1]]
+            rows_of += [jnp.concatenate([x0, zero], axis=1), jnp.concatenate([zero, x1], axis=1)]
+        lhs = jnp.concatenate(rows_of, axis=0).astype(BF16)
+        rhs = jnp.concatenate(
+            [jnp.concatenate([a_vm[m, i], a_vm[m, i + 1]], axis=0) for i in (t, t + 2)], axis=1
+        )
+        out = jnp.dot(lhs, rhs, preferred_element_type=F32)
+        return jnp.concatenate([out[0:16, 0:TILE], out[16:32, TILE:]], axis=0)
+
     def pair_product(m, t):
-        x0, x1 = xf[cols[t]], xf[cols[t + 1]]
+        x0, x1 = xf[m, cols[t]], xf[m, cols[t + 1]]
         lhs = jnp.concatenate(
             [jnp.concatenate([x0, zero], axis=1), jnp.concatenate([zero, x1], axis=1)], axis=0
         ).astype(BF16)
@@ -187,24 +202,42 @@
         return carry
 
     def run_last(k):
-        for p in range(PER // 2):
-            part = slice(16 * p, 16 * p + 16)
-            ysend[k, part, :] = (acc[k, part, :] + pair_product(2, k * PER + 2 * p)).astype(BF16)
-
-    for h in hops:
+        for p in range(PER // 4):
+            part = slice(32 * p, 32 * p + 32)
+            ysend[k, part, :] = (acc[k, part, :] + products(2, k * PER + 4 * p)).astype(BF16)
+
+    def unpack(m, slot):
+        xf[m, pl.ds(slot * REGION, REGION)] = xb[slot, m].astype(F32).reshape(REGION, BS, TILE)
+
+    def flip(m, q):
+        tile_copies[3 * m + q].wait()
+
+        def some(i, carry):
+            for u in range(16):
+                t = 64 * q + 16 * i + u
+                a_vm[m, t] = a_vm[m, t].T
+            return carry
+
+        lax.fori_loop(0, 4, some, 0)
+
+    for m, h in enumerate(hops):
         h[0].wait_recv()
         h[3].start()
         h[1].wait_recv()
         h[4].start()
-    for h in hops:
+    for m, h in enumerate(hops):
         h[2].wait_recv()
         h[5].start()
         h[6].start()
-    for h in hops:
+        for slot in (row, xh * 4 + down, xh * 4 + up, other * 4 + y):
+            unpack(m, slot)
+    for m, h in enumerate(hops):
         h[3].wait_recv()
         h[7].start()
         h[4].wait_recv()
         h[8].start()
+        unpack(m, xh * 4 + far)
+        flip(2, m)
 
     for copy in id_copies:
         copy.wait_recv()
@@ -215,8 +248,12 @@
         rf[k, PER * BS :, :] = jnp.zeros(((SLOTS - PER) * BS, TILE), F32)
 
     arrive(0)
+    for copy in tile_copies[0:3]:
+        copy.wait()
     lax.fori_loop(0, COLS, run_first, 0, unroll=COLS)
     arrive(1)
+    for copy in tile_copies[3:6]:
+        copy.wait()
     lax.fori_loop(0, COLS, run_second, 0, unroll=COLS)
 
     arrive(2)
@@ -225,12 +262,16 @@
         device, k = col_peer(j)
         return remote(ysend.at[k], yrecv.at[col], y_send.at[j], y_recv.at[j], device)
 
-    def last(j, carry):
+    def far_first(i):
+        return (1 - (i // 2) % 2) * 8 + (1 + i // 4) % 4 * 2 + 1 - i % 2
+
+    def last(i, carry):
+        j = far_first(i)
         run_last(col_peer(j)[1])
         result_copy(j).start()
         return carry
 
-    lax.fori_loop(1, COLS, last, 0, unroll=COLS - 1)
+    lax.fori_loop(0, COLS - 1, last, 0, unroll=COLS - 1)
     run_last(col)
 
     for copy in c1_copies:
@@ -247,13 +288,14 @@
 
     rf[col, 0 : PER * BS, :] = ysend[col].astype(F32)
 
-    def landed(j, carry):
+    def landed(i, carry):
+        j = far_first(i)
         k = col_source(j)
         result_copy(j).wait_recv()
         rf[k, 0 : PER * BS, :] = yrecv[k].astype(F32)
         return carry
 
-    lax.fori_loop(1, COLS, landed, 0, unroll=COLS - 1)
+    lax.fori_loop(0, COLS - 1, landed, 0, unroll=COLS - 1)
 
     for b in range(0, BS, 2):
         pair = [
@@ -270,7 +312,7 @@
     m1[col, :, 0:STACK] = (inner[16:24] + inner[8:16]) + inner[0:8]
     m1[col, :, STACK:] = jnp.zeros((BS, TILE - STACK), F32)
     m1_copies = []
-    for j in range(1, COLS):
+    for j in COL_ORDER:
         device, _ = col_peer(j)
         copy = remote(m1.at[col], m1.at[col], m1_send.at[j], m1_recv.at[j], device)
         copy.start()
@@ -285,14 +327,14 @@
     for i in range(3):
         cw[16 * i : 16 * i + 16, :] = jnp.where(keep, full if i == 0 else pltpu.roll(full, TILE - 40 * i, 1), 0.0)
     entries = float(st.shape[1] * ROWS * COLS)
-    corr = cw[:, 0:KP] * (1.0 / entries)
+    corr = cw[...] * (1.0 / entries)
     eye = jnp.where(
-        lax.broadcasted_iota(jnp.int32, (KP, KP), 0) == lax.broadcasted_iota(jnp.int32, (KP, KP), 1), 1.0, 0.0
+        lax.broadcasted_iota(jnp.int32, (KP, TILE), 0) == lax.broadcasted_iota(jnp.int32, (KP, TILE), 1), 1.0, 0.0
     ).astype(F32)
     dot = functools.partial(jnp.dot, precision=lax.Precision.HIGHEST, preferred_element_type=F32)
-    corr2 = dot(corr, corr)
-    pq[0] = 2.0 * eye - corr
-    pq[1] = 4.0 * eye - 6.0 * corr + 4.0 * corr2 - dot(corr2, corr)
+    corr2 = dot(corr[:, 0:KP], corr)
+    corr3 = dot(corr2[:, 0:KP], corr)
+    pq[...] = (2.0 * eye - corr) + pltpu.roll(4.0 * eye - 6.0 * corr + 4.0 * corr2 - corr3, TILE // 2, 1)
 
     for copy in m1_copies:
         copy.wait_recv()
@@ -301,7 +343,7 @@
         half = half + m1[k]
     m2[row] = half
     m2_copies = []
-    for j in range(1, ROWS):
+    for j in ROW_ORDER:
         copy = remote(m2.at[row], m2.at[row], m2_send.at[j], m2_recv.at[j], row_peer(j))
         copy.start()
         m2_copies.append(copy)
@@ -327,33 +369,43 @@
 
 def final_kernel(st, total, pq, new_block, coefficients, factor, *, entries):
     inverse_root = 1.0 / math.sqrt(entries)
-    dot = functools.partial(lax.dot_general, precision=lax.Precision.HIGHEST, preferred_element_type=F32)
-    nn = (((1,), (0,)), ((), ()))
     tot = total[...]
-    raw = tot[:, 0:KP] * inverse_root
-    energy = (
-        pltpu.roll(tot, TILE - KP, 1) + pltpu.roll(tot, TILE - KP - 8, 1) + pltpu.roll(tot, TILE - KP - 16, 1)
-    )[:, 0:BS]
-    coef = dot(raw, pq[0], nn)
-    gram = (energy - dot(dot(raw, pq[1], nn), raw, NT)) * (1.0 / entries)
-    coefficients[...] = coef[:, 0:KD]
+    raw = tot * inverse_root
+    both = jnp.dot(raw[:, 0:KP], pq[...], precision=lax.Precision.HIGHEST, preferred_element_type=F32)
+    coefficients[...] = both[:, 0:KD]
 
     sub = lax.broadcasted_iota(jnp.int32, (BS, TILE), 0)
     lane = lax.broadcasted_iota(jnp.int32, (BS, TILE), 1)
-    unit = (lane == sub + KP) | (lane == sub + KP + 8) | (lane == sub + KP + 16)
-    target = jnp.where(unit, 1.0, 0.0).astype(F32)
-    target = target + jnp.concatenate([coef * -inverse_root, jnp.zeros((BS, TILE - KP), F32)], axis=1)
-    left = jnp.concatenate([gram, jnp.zeros((BS, TILE - BS), F32)], axis=1)
+    basis_part = lane < KP
+    turned = jnp.where(basis_part, pltpu.roll(both, TILE // 2, 1), 0.0)
+
+    def parts_of(index):
+        return (lane == index + KP) | (lane == index + KP + 8) | (lane == index + KP + 16)
+
+    def spread(value, j):
+        return jnp.broadcast_to(value[j : j + 1, :], (BS, TILE))
+
+    columns = [
+        jnp.broadcast_to(
+            jnp.sum(jnp.where(parts_of(j), tot, 0.0) - turned * spread(raw, j), axis=1, keepdims=True)
+            * (1.0 / entries),
+            (BS, TILE),
+        )
+        for j in range(BS)
+    ]
+    target = jnp.where(basis_part, both * -inverse_root, 0.0) + jnp.where(parts_of(sub), 1.0, 0.0)
     lower = jnp.zeros((BS, TILE), F32)
     for j in range(BS):
-        root = jnp.sqrt(left[j : j + 1, j : j + 1])
-        scale = jnp.broadcast_to(1.0 / root, (BS, 1))
-        column = jnp.broadcast_to(left[:, j : j + 1] * scale, (BS, TILE))
+        pivot = spread(columns[j], j)
+        scale = lax.rsqrt(pivot)
+        scale = scale * (1.5 - 0.5 * pivot * scale * scale)
+        column = columns[j] * scale
         below = jnp.where(sub > j, column, 0.0)
         lower = jnp.where((lane == j) & (sub >= j), column, lower)
-        solved = jnp.broadcast_to(target[j : j + 1, :], (BS, TILE)) * scale
+        solved = spread(target, j) * scale
         target = jnp.where(sub == j, solved, target - below * solved)
-        left = left - below * (jnp.broadcast_to(left[j : j + 1, :], (BS, TILE)) * scale)
+        for i in range(j + 1, BS):
+            columns[i] = columns[i] - below * spread(below, i)
     factor[...] = lower[:, 0:BS]
     mix = jnp.concatenate(split3(target[:, 0:STACK]), axis=0).astype(BF16)
     length = st.shape[1]
@@ -373,7 +425,7 @@
         out_shape=(
             jax.ShapeDtypeStruct((STACK, length), BF16),
             jax.ShapeDtypeStruct((BS, TILE), F32),
-            jax.ShapeDtypeStruct((2, KP, KP), F32),
+            jax.ShapeDtypeStruct((KP, TILE), F32),
         ),
         in_specs=[hbm] * 5,
         out_specs=(vmem, vmem, vmem),
@@ -384,7 +436,7 @@
             pltpu.SMEM(tile_cols.shape, jnp.int32),
             pltpu.VMEM(tiles.shape, BF16),
             pltpu.VMEM((ROWS, MATS, 256, TILE), BF16),
-            pltpu.VMEM((ROWS * REGION, BS, TILE), F32),
+            pltpu.VMEM((MATS, ROWS * REGION, BS, TILE), F32),
             pltpu.VMEM((COLS, PER * BS, TILE), F32),
             pltpu.VMEM((COLS, PER * BS, TILE), BF16),
             pltpu.VMEM((COLS, PER * BS, TILE), BF16),
@@ -399,7 +451,7 @@
             pltpu.VMEM((ROWS, BS, TILE), F32),
             pltpu.VMEM((KP, TILE), F32),
             dma((4,)),
-            dma((MATS, 4)),
+            dma((MATS, 3)),
             dma((MATS, 9)), dma((MATS, 9)),
             dma((COLS,)), dma((COLS,)),
             dma((COLS,)), dma((COLS,)),

time: 46.2 us -> 44.5 us (0.963)
  Pallas kernels: 45.4 us -> 43.7 us
    pallas_call x1, Pallas kernels: 43.3 us -> 42.4 us  [shards(): pl.pallas_call(step_kernel, out_shape=(jax.ShapeDtypeStruct((STACK, lengt...]
    pallas_call x1, Pallas kernels: 2.12 us -> 1.33 us  [shards(): pl.pallas_call(functools.partial(final_kernel, entries=length * ROWS * CO...]
where the time goes in v3:
time: 44.5 us; the launch traced here: 44.4 us
  Pallas kernels  43.7 us (98%)
  between operations  0.64 us (1%)
    pallas_call x1, Pallas kernels, shards(): pl.pallas_call(step_kernel, out_shape=(jax.ShapeDtypeStruct((STACK, lengt...  42.4 us
    pallas_call x1, Pallas kernels, shards(): pl.pallas_call(functools.partial(final_kernel, entries=length * ROWS * CO...  1.33 us

profile of v3, /device:TPU:1, one launch (start us, length us, event | category | flops | bytes accessed | tf_op | source)
XLA Modules:
  0.0 44.4 jit_solution(16375244587292874665)
XLA Ops:
  0.6 42.4 %toar_step.1 = (bf16[80,4096]{1,0:T(8,128)(2,1)S(1)}, f32[8,128]{1,0:T(8,128)S(1)}, f32[48,128]{1,0:T(8,128)S(1)}) custom-call(bf16[40,4096]{1,0:T(8,128)(2,1)} %basis_hbm.1, f32[3,8,40]{2,1,0:T(8,128)} %expand_hbm.1, s32[192]{0:T(256)} %rows_hbm.1, s32[192]{0:T(256)} %cols_hbm.1, bf16[3,192,128,128]{3,2,1,0:T(8,128)(2,1)} %tiles.1), custom_call_target="tpu_custom_call" | custom-call | tf_op jit(solution)/shard_map/toar_step/pallas_call | solution.py:423
  43.0 1.3 %toar_final.1 = (f32[8,4096]{1,0:T(8,128)}, f32[8,40]{1,0:T(8,128)}, f32[8,8]{1,0:T(8,128)}) custom-call(bf16[80,4096]{1,0:T(8,128)(2,1)S(1)} %get-tuple-element.6.st, f32[8,128]{1,0:T(8,128)S(1)} %get-tuple-element.7.total, f32[48,128]{1,0:T(8,128)S(1)} %get-tuple-element.8.pq), custom_call_target="tpu_custom_call" | custom-call | tf_op jit(solution)/shard_map/toar_final/pallas_call | solution.py:469

commit v4 on v3

--- a/solution.py
+++ b/solution.py
@@ -46,9 +46,8 @@
         px, pz, pk = lax.rem(xl + j // 8, 2), lax.rem(z + (j // 2) % 4, 4), lax.rem(core + j % 2, 2)
         return (xh, y, px, pz, pk), px * 8 + pz * 2 + pk
 
-    def col_source(j):
-        px, pz, pk = lax.rem(xl + j // 8, 2), lax.rem(z + 4 - (j // 2) % 4, 4), lax.rem(core + j % 2, 2)
-        return px * 8 + pz * 2 + pk
+    def far_first(i):
+        return (1 - (i // 2) % 2) * 8 + (1 + i // 4) % 4 * 2 + 1 - i % 2
 
     def row_peer(j):
         ph, py = lax.rem(xh + j // 4, 2), lax.rem(y + j % 4, 4)
@@ -139,12 +138,12 @@
 
     lax.fori_loop(0, COLS, fill_ids, 0)
     id_copies = []
-    for j in range(1, COLS):
-        device, k = col_peer(j)
-        copy = remote(ids_s.at[k], ids_r.at[col], i_send.at[j], i_recv.at[j], device)
+    for i in range(COLS - 1):
+        device, k = col_peer(far_first(i))
+        copy = remote(ids_s.at[k], ids_r.at[i], i_send.at[i], i_recv.at[i], device)
         copy.start()
         id_copies.append(copy)
-    ids_r[col] = ids_s[col]
+    ids_r[COLS - 1] = ids_s[col]
 
     st[0:KD, :] = basis[...]
     st[KD:KP, :] = jnp.zeros((KP - KD, st.shape[1]), BF16)
@@ -192,8 +191,8 @@
         return lax.dot_general(lhs, rhs, NT, preferred_element_type=F32)
 
     def run_first(k, carry):
-        for p in range(PER // 2):
-            acc[k, 16 * p : 16 * p + 16, :] = pair_product(0, k * PER + 2 * p)
+        for p in range(PER // 4):
+            acc[k, 32 * p : 32 * p + 32, :] = products(0, k * PER + 4 * p)
         return carry
 
     def run_second(k, carry):
@@ -213,18 +212,19 @@
         tile_copies[3 * m + q].wait()
 
         def some(i, carry):
-            for u in range(16):
-                t = 64 * q + 16 * i + u
+            for u in range(32):
+                t = 64 * q + 32 * i + u
                 a_vm[m, t] = a_vm[m, t].T
             return carry
 
-        lax.fori_loop(0, 4, some, 0)
+        lax.fori_loop(0, 2, some, 0)
 
     for m, h in enumerate(hops):
         h[0].wait_recv()
         h[3].start()
         h[1].wait_recv()
         h[4].start()
+        flip(0, m)
     for m, h in enumerate(hops):
         h[2].wait_recv()
         h[5].start()
@@ -248,8 +248,6 @@
         rf[k, PER * BS :, :] = jnp.zeros(((SLOTS - PER) * BS, TILE), F32)
 
     arrive(0)
-    for copy in tile_copies[0:3]:
-        copy.wait()
     lax.fori_loop(0, COLS, run_first, 0, unroll=COLS)
     arrive(1)
     for copy in tile_copies[3:6]:
@@ -258,17 +256,13 @@
 
     arrive(2)
 
-    def result_copy(j):
-        device, k = col_peer(j)
-        return remote(ysend.at[k], yrecv.at[col], y_send.at[j], y_recv.at[j], device)
-
-    def far_first(i):
-        return (1 - (i // 2) % 2) * 8 + (1 + i // 4) % 4 * 2 + 1 - i % 2
+    def result_copy(i):
+        device, k = col_peer(far_first(i))
+        return remote(ysend.at[k], yrecv.at[i], y_send.at[i], y_recv.at[i], device)
 
     def last(i, carry):
-        j = far_first(i)
-        run_last(col_peer(j)[1])
-        result_copy(j).start()
+        run_last(col_peer(far_first(i))[1])
+        result_copy(i).start()
         return carry
 
     lax.fori_loop(0, COLS - 1, last, 0, unroll=COLS - 1)
@@ -286,24 +280,30 @@
         copy.start()
         c2_copies.append(copy)
 
-    rf[col, 0 : PER * BS, :] = ysend[col].astype(F32)
+    rf[COLS - 1, 0 : PER * BS, :] = ysend[col].astype(F32)
 
     def landed(i, carry):
-        j = far_first(i)
-        k = col_source(j)
-        result_copy(j).wait_recv()
-        rf[k, 0 : PER * BS, :] = yrecv[k].astype(F32)
-        return carry
-
-    lax.fori_loop(0, COLS - 1, landed, 0, unroll=COLS - 1)
-
-    for b in range(0, BS, 2):
-        pair = [
-            jnp.concatenate([rf[k, pl.ds(b + i, SLOTS, stride=BS), :] for k in range(COLS)], axis=0) for i in range(2)
-        ]
-        both = jnp.dot(onehot[...], jnp.concatenate(pair, axis=1).astype(BF16), preferred_element_type=F32)
-        for i in range(2):
-            app[pl.ds(b + i, REGION, stride=BS), :] = both[:, i * TILE : (i + 1) * TILE]
+        result_copy(i).wait_recv()
+        rf[i, 0 : PER * BS, :] = yrecv[i].astype(F32)
+        return carry
+
+    half_cols = COLS // 2
+    for g in range(2):
+        lax.fori_loop(g * half_cols, min((g + 1) * half_cols, COLS - 1), landed, 0, unroll=half_cols - g)
+        group = range(g * half_cols, (g + 1) * half_cols)
+        for b in range(0, BS, 2):
+            pair = [
+                jnp.concatenate([rf[k, pl.ds(b + i, SLOTS, stride=BS), :] for k in group], axis=0) for i in range(2)
+            ]
+            both = jnp.dot(
+                onehot[:, g * half_cols * SLOTS : (g + 1) * half_cols * SLOTS],
+                jnp.concatenate(pair, axis=1).astype(BF16),
+                preferred_element_type=F32,
+            )
+            for i in range(2):
+                value = both[:, i * TILE : (i + 1) * TILE]
+                place = pl.ds(b + i, REGION, stride=BS)
+                app[place, :] = value if g == 0 else app[place, :] + value
     for s in range(REGION):
         parts = split3(app[s * BS : (s + 1) * BS, :])
         st[KP:STACK, s * TILE : (s + 1) * TILE] = jnp.concatenate([*parts, zero], axis=0).astype(BF16)
@@ -360,11 +360,11 @@
     for copy in (*id_copies, *c1_copies, *c2_copies, *m1_copies, *m2_copies):
         copy.wait_send()
 
-    def sent(j, carry):
-        result_copy(j).wait_send()
-        return carry
-
-    lax.fori_loop(1, COLS, sent, 0)
+    def sent(i, carry):
+        result_copy(i).wait_send()
+        return carry
+
+    lax.fori_loop(0, COLS - 1, sent, 0)
 
 
 def final_kernel(st, total, pq, new_block, coefficients, factor, *, entries):

time: 44.5 us -> 43.8 us (0.984)
  Pallas kernels: 43.7 us -> 43 us
    pallas_call x1, Pallas kernels: 42.4 us -> 41.7 us  [shards(): pl.pallas_call(step_kernel, out_shape=(jax.ShapeDtypeStruct((STACK, lengt...]
where the time goes in v4:
time: 43.8 us; the launch traced here: 43.6 us
  Pallas kernels  43 us (98%)
  between operations  0.64 us (1%)
    pallas_call x1, Pallas kernels, shards(): pl.pallas_call(step_kernel, out_shape=(jax.ShapeDtypeStruct((STACK, lengt...  41.7 us
    pallas_call x1, Pallas kernels, shards(): pl.pallas_call(functools.partial(final_kernel, entries=length * ROWS * CO...  1.33 us

profile of v4, /device:TPU:1, one launch (start us, length us, event | category | flops | bytes accessed | tf_op | source)
XLA Modules:
  0.0 43.6 jit_solution(1422931742092754651)
XLA Ops:
  0.6 41.7 %toar_step.1 = (bf16[80,4096]{1,0:T(8,128)(2,1)S(1)}, f32[8,128]{1,0:T(8,128)S(1)}, f32[48,128]{1,0:T(8,128)S(1)}) custom-call(bf16[40,4096]{1,0:T(8,128)(2,1)} %basis_hbm.1, f32[3,8,40]{2,1,0:T(8,128)} %expand_hbm.1, s32[192]{0:T(256)} %rows_hbm.1, s32[192]{0:T(256)} %cols_hbm.1, bf16[3,192,128,128]{3,2,1,0:T(8,128)(2,1)} %tiles.1), custom_call_target="tpu_custom_call" | custom-call | tf_op jit(solution)/shard_map/toar_step/pallas_call | solution.py:423
  42.3 1.3 %toar_final.1 = (f32[8,4096]{1,0:T(8,128)}, f32[8,40]{1,0:T(8,128)}, f32[8,8]{1,0:T(8,128)}) custom-call(bf16[80,4096]{1,0:T(8,128)(2,1)S(1)} %get-tuple-element.6.st, f32[8,128]{1,0:T(8,128)S(1)} %get-tuple-element.7.total, f32[48,128]{1,0:T(8,128)S(1)} %get-tuple-element.8.pq), custom_call_target="tpu_custom_call" | custom-call | tf_op jit(solution)/shard_map/toar_final/pallas_call | solution.py:469

commit v5 on v4

--- a/solution.py
+++ b/solution.py
@@ -67,10 +67,10 @@
     for copy in in_copies:
         copy.start()
     barrier = pltpu.get_barrier_semaphore()
-    for j in range(1, ROWS):
+    for j in ROW_ORDER:
         pl.semaphore_signal(barrier, inc=1, device_id=row_peer(j), device_id_type=MESH)
-    for j in range(1, COLS):
-        pl.semaphore_signal(barrier, inc=1, device_id=col_peer(j)[0], device_id_type=MESH)
+    for i in range(COLS - 1):
+        pl.semaphore_signal(barrier, inc=1, device_id=col_peer(far_first(i))[0], device_id_type=MESH)
 
     in_copies[0].wait()
     in_copies[1].wait()
@@ -152,59 +152,6 @@
     cw[:, 0:KP] = own
     packed = cw[0:16, :] + pltpu.roll(cw[16:32, :], 40, 1) + pltpu.roll(cw[32:48, :], 80, 1)
     c1[col] = packed
-    c1_copies = []
-    for j in range(1, COLS):
-        device, _ = col_peer(j)
-        copy = remote(c1.at[col], c1.at[col], c1_send.at[j], c1_recv.at[j], device)
-        copy.start()
-        c1_copies.append(copy)
-
-    def arrive(m):
-        hops[m][5].wait_recv()
-        unpack(m, other * 4 + down)
-        hops[m][6].wait_recv()
-        unpack(m, other * 4 + up)
-        hops[m][7].wait_recv()
-        hops[m][8].wait_recv()
-        unpack(m, other * 4 + far)
-
-    zero = jnp.zeros((BS, TILE), F32)
-
-    def products(m, t):
-        rows_of = []
-        for i in (t, t + 2):
-            x0, x1 = xf[m, cols[i]], xf[m, cols[i + 1]]
-            rows_of += [jnp.concatenate([x0, zero], axis=1), jnp.concatenate([zero, x1], axis=1)]
-        lhs = jnp.concatenate(rows_of, axis=0).astype(BF16)
-        rhs = jnp.concatenate(
-            [jnp.concatenate([a_vm[m, i], a_vm[m, i + 1]], axis=0) for i in (t, t + 2)], axis=1
-        )
-        out = jnp.dot(lhs, rhs, preferred_element_type=F32)
-        return jnp.concatenate([out[0:16, 0:TILE], out[16:32, TILE:]], axis=0)
-
-    def pair_product(m, t):
-        x0, x1 = xf[m, cols[t]], xf[m, cols[t + 1]]
-        lhs = jnp.concatenate(
-            [jnp.concatenate([x0, zero], axis=1), jnp.concatenate([zero, x1], axis=1)], axis=0
-        ).astype(BF16)
-        rhs = jnp.concatenate([a_vm[m, t], a_vm[m, t + 1]], axis=1)
-        return lax.dot_general(lhs, rhs, NT, preferred_element_type=F32)
-
-    def run_first(k, carry):
-        for p in range(PER // 4):
-            acc[k, 32 * p : 32 * p + 32, :] = products(0, k * PER + 4 * p)
-        return carry
-
-    def run_second(k, carry):
-        for p in range(PER // 2):
-            acc[k, 16 * p : 16 * p + 16, :] += pair_product(1, k * PER + 2 * p)
-        return carry
-
-    def run_last(k):
-        for p in range(PER // 4):
-            part = slice(32 * p, 32 * p + 32)
-            ysend[k, part, :] = (acc[k, part, :] + products(2, k * PER + 4 * p)).astype(BF16)
-
     def unpack(m, slot):
         xf[m, pl.ds(slot * REGION, REGION)] = xb[slot, m].astype(F32).reshape(REGION, BS, TILE)
 
@@ -238,6 +185,59 @@
         h[8].start()
         unpack(m, xh * 4 + far)
         flip(2, m)
+
+    c1_copies = []
+    for j in range(1, COLS):
+        device, _ = col_peer(j)
+        copy = remote(c1.at[col], c1.at[col], c1_send.at[j], c1_recv.at[j], device)
+        copy.start()
+        c1_copies.append(copy)
+
+    def arrive(m):
+        hops[m][5].wait_recv()
+        unpack(m, other * 4 + down)
+        hops[m][6].wait_recv()
+        unpack(m, other * 4 + up)
+        hops[m][7].wait_recv()
+        hops[m][8].wait_recv()
+        unpack(m, other * 4 + far)
+
+    zero = jnp.zeros((BS, TILE), F32)
+
+    def products(m, t):
+        rows_of = []
+        for i in (t, t + 2):
+            x0, x1 = xf[m, cols[i]], xf[m, cols[i + 1]]
+            rows_of += [jnp.concatenate([x0, zero], axis=1), jnp.concatenate([zero, x1], axis=1)]
+        lhs = jnp.concatenate(rows_of, axis=0).astype(BF16)
+        rhs = jnp.concatenate(
+            [jnp.concatenate([a_vm[m, i], a_vm[m, i + 1]], axis=0) for i in (t, t + 2)], axis=1
+        )
+        out = jnp.dot(lhs, rhs, preferred_element_type=F32)
+        return jnp.concatenate([out[0:16, 0:TILE], out[16:32, TILE:]], axis=0)
+
+    def pair_product(m, t):
+        x0, x1 = xf[m, cols[t]], xf[m, cols[t + 1]]
+        lhs = jnp.concatenate(
+            [jnp.concatenate([x0, zero], axis=1), jnp.concatenate([zero, x1], axis=1)], axis=0
+        ).astype(BF16)
+        rhs = jnp.concatenate([a_vm[m, t], a_vm[m, t + 1]], axis=1)
+        return lax.dot_general(lhs, rhs, NT, preferred_element_type=F32)
+
+    def run_first(k, carry):
+        for p in range(PER // 4):
+            acc[k, 32 * p : 32 * p + 32, :] = products(0, k * PER + 4 * p)
+        return carry
+
+    def run_second(k, carry):
+        for p in range(PER // 2):
+            acc[k, 16 * p : 16 * p + 16, :] += pair_product(1, k * PER + 2 * p)
+        return carry
+
+    def run_last(k):
+        for p in range(PER // 4):
+            part = slice(32 * p, 32 * p + 32)
+            ysend[k, part, :] = (acc[k, part, :] + products(2, k * PER + 4 * p)).astype(BF16)
 
     for copy in id_copies:
         copy.wait_recv()

time: 43.8 us -> 43.4 us (level)
  no operation moved by 1% of the time
where the time goes in v5:
time: 43.4 us; the launch traced here: 43.3 us
  Pallas kernels  42.7 us (98%)
  between operations  0.64 us (1%)
    pallas_call x1, Pallas kernels, shards(): pl.pallas_call(step_kernel, out_shape=(jax.ShapeDtypeStruct((STACK, lengt...  41.3 us
    pallas_call x1, Pallas kernels, shards(): pl.pallas_call(functools.partial(final_kernel, entries=length * ROWS * CO...  1.33 us

profile of v5, /device:TPU:1, one launch (start us, length us, event | category | flops | bytes accessed | tf_op | source)
XLA Modules:
  0.0 43.3 jit_solution(1702432573723495406)
XLA Ops:
  0.6 41.3 %toar_step.1 = (bf16[80,4096]{1,0:T(8,128)(2,1)S(1)}, f32[8,128]{1,0:T(8,128)S(1)}, f32[48,128]{1,0:T(8,128)S(1)}) custom-call(bf16[40,4096]{1,0:T(8,128)(2,1)} %basis_hbm.1, f32[3,8,40]{2,1,0:T(8,128)} %expand_hbm.1, s32[192]{0:T(256)} %rows_hbm.1, s32[192]{0:T(256)} %cols_hbm.1, bf16[3,192,128,128]{3,2,1,0:T(8,128)(2,1)} %tiles.1), custom_call_target="tpu_custom_call" | custom-call | tf_op jit(solution)/shard_map/toar_step/pallas_call | solution.py:423
  42.0 1.3 %toar_final.1 = (f32[8,4096]{1,0:T(8,128)}, f32[8,40]{1,0:T(8,128)}, f32[8,8]{1,0:T(8,128)}) custom-call(bf16[80,4096]{1,0:T(8,128)(2,1)S(1)} %get-tuple-element.6.st, f32[8,128]{1,0:T(8,128)S(1)} %get-tuple-element.7.total, f32[48,128]{1,0:T(8,128)S(1)} %get-tuple-element.8.pq), custom_call_target="tpu_custom_call" | custom-call | tf_op jit(solution)/shard_map/toar_final/pallas_call | solution.py:469
